TPU v7x, 128 devices: a whole 4x4x4 slice. The times are simulated.
128 devices in a mesh: row: 16 (over y, z_hi, core), col: 8 (over x, z_lo).
Axes of the slice: x: 4, y: 4, z: 4 (z_hi: 2, z_lo: 2; z = z_hi * 2 + z_lo), core: 2. Of those that a mesh axis runs over, the one named last changes fastest.
Arguments:
- homolog_embedding: bfloat16 [128, 1024, 64], P(('row', 'col')), may hold values from -6 to 6
- split_mapping_matrix: bfloat16 [64, 64], replicated, may hold values from -0.75 to 0.75
- couple_mapping_matrix: bfloat16 [1024, 128], replicated, may hold values from -1.5 to 1.5
- couple_offset_vector: bfloat16 [128], replicated, may hold values from -3 to 3
- incoming_adjoint_couple: bfloat16 [1024, 1024, 128], P('row', 'col'), may hold values from -0.29882812 to 0.29882812
Outputs:
- pair_delta_output: bfloat16 [1024, 1024, 128], P('row', 'col')
- alignment_gradient: bfloat16 [128, 1024, 64], P(('row', 'col'))
- out_weight_grad: float32 [1024, 128], replicated
All inputs are finite; a program needn't handle non-finite values.
Results may differ from a plain program's by a relative error of at most 0.015.
Values may be sent and summed in bfloat16 or wider, within the bound.
A program may use at most 64 MiB of HBM per device.

v0:
```python
import math
import jax
import jax.numpy as jnp
from jax import lax
from jax.sharding import PartitionSpec as P


def copy_for_each(array, axis):
    size = lax.axis_size(axis)
    return lax.all_to_all(
        jnp.broadcast_to(array[None], (size, *array.shape)), axis, 0, 0, tiled=True
    )


def laid_out(pieces, dim):
    pieces = jnp.moveaxis(pieces, 0, dim)
    shape = pieces.shape
    return pieces.reshape(*shape[:dim], shape[dim] * shape[dim + 1], *shape[dim + 2 :])


def gather_directly(array, axis, dim):
    pieces = copy_for_each(array, axis)
    return laid_out(pieces, dim)


def cut_along(array, dim, size):
    before, after = (array.shape[:dim], array.shape[dim + 1 :])
    return jnp.moveaxis(array.reshape(*before, size, -1, *after), dim, 0)


def summed_on_arrival(array, axis, dim):
    size = lax.axis_size(axis)
    pieces = lax.all_to_all(cut_along(array, dim, size), axis, 0, 0, tiled=True)
    return jnp.sum(pieces.astype(jnp.float32), axis=0)


def standardize_features(homolog_embedding):
    mapped_halves = homolog_embedding.astype(jnp.float32)
    center = jnp.mean(mapped_halves, axis=-1, keepdims=True)
    spread = jnp.mean((mapped_halves - center) * (mapped_halves - center), axis=-1, keepdims=True)
    reciprocal_spread = lax.rsqrt(spread + 1e-05)
    return ((mapped_halves - center) * reciprocal_spread, reciprocal_spread)


def regroup(mapped_halves, outer_count, inner_count):
    shaped = mapped_halves.reshape((outer_count, inner_count, -1) + mapped_halves.shape[1:])
    return jnp.swapaxes(shaped, 0, 1).reshape(mapped_halves.shape)


def on_device(
    homolog_embedding,
    split_mapping_matrix,
    couple_mapping_matrix,
    couple_offset_vector,
    incoming_adjoint_couple,
):
    rows_count = lax.axis_size("row")
    cols_count = lax.axis_size("col")
    width = split_mapping_matrix.shape[1] // 2
    standardized_activations, reciprocal_spread = standardize_features(homolog_embedding)
    normalized_input = standardized_activations.astype(jnp.bfloat16)
    factors = jnp.dot(
        normalized_input, split_mapping_matrix, preferred_element_type=jnp.float32
    ).astype(jnp.bfloat16)
    left = factors[..., :width]
    right = factors[..., width:]
    left_part = lax.all_to_all(left, "row", split_axis=1, concat_axis=0, tiled=True)
    left_panel = regroup(gather_directly(left_part, "col", 0), cols_count, rows_count)
    right_part = lax.all_to_all(right, "col", split_axis=1, concat_axis=0, tiled=True)
    right_panel = gather_directly(right_part, "row", 0)
    seq_total = left_panel.shape[0]
    rows_local = left_panel.shape[1]
    cols_local = right_panel.shape[1]
    channels = incoming_adjoint_couple.shape[2]
    step_rows = math.gcd(rows_local, 16)
    count = rows_local // step_rows
    left_blocks = left_panel.reshape(seq_total, count, step_rows, width).transpose(1, 0, 2, 3)
    cot_blocks = incoming_adjoint_couple.reshape(count, step_rows, cols_local, channels)
    bias_wide = couple_offset_vector.astype(jnp.float32)
    weight_back = couple_mapping_matrix.T

    def advance(carry, inputs):
        weight_sum, right_sum = carry
        left_block, cot_block = inputs
        outer = (
            jnp.einsum("sic,sje->ijce", left_block, right_panel, preferred_element_type=jnp.float32)
            / seq_total
        )
        flat = outer.astype(jnp.bfloat16).reshape(step_rows * cols_local, width * width)
        update = (
            jnp.dot(flat, couple_mapping_matrix, preferred_element_type=jnp.float32) + bias_wide
        ).astype(jnp.bfloat16)
        grad_rows = cot_block.reshape(step_rows * cols_local, channels)
        outer_grad = jnp.dot(grad_rows, weight_back, preferred_element_type=jnp.float32).astype(
            jnp.bfloat16
        )
        outer_grad = outer_grad.reshape(step_rows, cols_local, width, width)
        weight_sum = weight_sum + lax.dot_general(
            flat, grad_rows, (((0,), (0,)), ((), ())), preferred_element_type=jnp.float32
        )
        left_grad = (
            jnp.einsum("ijce,sje->sic", outer_grad, right_panel, preferred_element_type=jnp.float32)
            / seq_total
        )
        right_sum = (
            right_sum
            + jnp.einsum(
                "ijce,sic->sje", outer_grad, left_block, preferred_element_type=jnp.float32
            )
            / seq_total
        )
        return (
            (weight_sum, right_sum),
            (update.reshape(step_rows, cols_local, channels), left_grad),
        )

    start = (
        jnp.zeros((width * width, channels), jnp.float32),
        jnp.zeros((seq_total, cols_local, width), jnp.float32),
    )
    (weight_part, right_grad), (updates, left_grads) = lax.scan(
        advance, start, (left_blocks, cot_blocks)
    )
    pair_delta_output = updates.reshape(rows_local, cols_local, channels)
    left_grad = left_grads.transpose(1, 0, 2, 3).reshape(seq_total, rows_local, width)
    left_summed = summed_on_arrival(
        regroup(left_grad, rows_count, cols_count).astype(jnp.bfloat16), "col", 0
    ).astype(jnp.bfloat16)
    left_back = lax.all_to_all(left_summed, "row", split_axis=0, concat_axis=1, tiled=True)
    right_summed = summed_on_arrival(right_grad.astype(jnp.bfloat16), "row", 0).astype(jnp.bfloat16)
    right_back = lax.all_to_all(right_summed, "col", split_axis=0, concat_axis=1, tiled=True)
    factor_weight_gradient = lax.psum(weight_part, ("row", "col"))
    both = jnp.concatenate([left_back, right_back], axis=-1)
    normalized_gradient = jnp.dot(both, split_mapping_matrix.T, preferred_element_type=jnp.float32)
    first_factor = jnp.mean(normalized_gradient, axis=-1, keepdims=True)
    second_factor = jnp.mean(normalized_gradient * standardized_activations, axis=-1, keepdims=True)
    alignment_gradient = (
        reciprocal_spread
        * (normalized_gradient - first_factor - standardized_activations * second_factor)
    ).astype(jnp.bfloat16)
    return (pair_delta_output, alignment_gradient, factor_weight_gradient)


def solution(mesh):
    placed = (P(("row", "col"), None, None), P(), P(), P(), P("row", "col", None))
    return jax.shard_map(
        on_device,
        mesh=mesh,
        in_specs=placed,
        out_specs=(P("row", "col", None), P(("row", "col"), None, None), P()),
        check_vma=False,
    )
```

profile of v0, /device:TPU:1, one launch (start us, length us, event | category | flops | bytes accessed | tf_op | source)
XLA Modules:
  0.0 425.5 jit_solution(13450894267339800620)
XLA Ops:
  11.2 2.3 reduce.7
  14.4 9.3 %all-to-all-start = ((bf16[16,2,1024]{2,1,0:T(2,128)(2,1)}), bf16[16,2,1024]{2,1,0:T(2,128)(2,1)S(1)}, u32[]{:S(2)}, u32[]{:S(2)}) async-start(bf16[16,2,1024]{2,1,0:T(2,128)(2,1)} %reshape.113), calls=%async_computation | async-start | bytes 131072 | tf_op jit(solution)/shard_map/all_to_all | solution.py:67
  24.0 2.3 reduce.8
  27.2 3.8 all-to-all-done
  31.0 4.5 %all-to-all-start.2 = ((bf16[8,2,2048]{2,1,0:T(2,128)(2,1)}), bf16[8,2,2048]{2,1,0:T(2,128)(2,1)S(1)}, u32[]{:S(2)}, u32[]{:S(2)}) async-start(bf16[8,2,2048]{2,1,0:T(2,128)(2,1)} %reshape.117), calls=%async_computation.2 | async-start | bytes 131072 | tf_op jit(solution)/shard_map/all_to_all | solution.py:69
  36.5 1.5 reshape.115
  38.0 2.6 all-to-all-done.2
  40.6 3.5 all-to-all-start.1
  44.8 7.0 %all-to-all-done.1 = bf16[8,2,16384]{2,1,0:T(2,128)(2,1)S(1)} async-done(((bf16[8,2,16384]{2,1,0:T(2,128)(2,1)}), bf16[8,2,16384]{2,1,0:T(2,128)(2,1)S(1)}, u32[]{:S(2)}, u32[]{:S(2)}) %all-to-all-start.1) | async-done | bytes 524320 | tf_op jit(solution)/shard_map/all_to_all | solution.py:10
  53.0 6.9 %all-to-all-start.3 = ((bf16[16,8,128,32]{2,1,3,0:T(8,128)(2,1)}), bf16[16,8,128,32]{2,1,3,0:T(8,128)(2,1)}, u32[]{:S(2)}, u32[]{:S(2)}) async-start(bf16[16,8,128,32]{2,1,3,0:T(8,128)(2,1)} %broadcast_in_dim.48), calls=%async_computation.3 | async-start | bytes 2097152 | tf_op jit(solution)/shard_map/all_to_all | solution.py:10
  60.0 1.6 reshape.116
  63.0 1.9 copy.40
  64.9 3.9 copy.45
  68.8 8.3 %all-to-all-done.3 = bf16[16,8,128,32]{2,1,3,0:T(8,128)(2,1)} async-done(((bf16[16,8,128,32]{2,1,3,0:T(8,128)(2,1)}), bf16[16,8,128,32]{2,1,3,0:T(8,128)(2,1)}, u32[]{:S(2)}, u32[]{:S(2)}) %all-to-all-start.3) | async-done | bytes 1048608 | tf_op jit(solution)/shard_map/all_to_all | solution.py:10
  78.9 128.3 %while.17 = (s32[]{:T(128)}, f32[1024,128]{1,0:T(8,128)}, f32[128,128,32]{1,0,2:T(8,128)S(1)}, bf16[4,16,128,128]{3,2,1,0:T(8,128)(2,1)}, bf16[4,128,16,32]{1,2,...) while((s32[]{:T(128)}, f32[1024,128]{1,0:T(8,128)}, ...), condition=%wide.region_3.4_spmd.clone, body=%wide.region_2.3_spmd.clone.sunk | while | flops 3229941760 | bytes 96995688 | solution.py:121
  79.1 2.3 fusion.88
  81.4 2.7 copy.91
  84.2 2.0 fusion.89
  86.2 1.9 constant_dynamic-update-slice_fusion.2
  88.1 3.5 fusion.90
  91.6 3.2 convolution_convert_fusion.3
  94.8 6.5 %copy.92 = bf16[2048,1024]{0,1:T(8,128)(2,1)} copy(bf16[2048,1024]{1,0:T(8,128)(2,1)} %convolution_convert_fusion.3) | data formatting | bytes 8388608 | tf_op jit(solution)/shard_map/while/body/eval_jaxpr/convert_element_type | solution.py:94
  101.3 3.6 copy.93
  104.9 4.1 fusion.91
  111.2 2.3 fusion.88
  113.4 2.7 copy.91
  116.2 2.0 fusion.89
  118.2 1.9 constant_dynamic-update-slice_fusion.2
  120.1 3.5 fusion.90
  123.6 3.2 convolution_convert_fusion.3
  126.8 6.5 %copy.92 = bf16[2048,1024]{0,1:T(8,128)(2,1)} copy(bf16[2048,1024]{1,0:T(8,128)(2,1)} %convolution_convert_fusion.3) | data formatting | bytes 8388608 | tf_op jit(solution)/shard_map/while/body/eval_jaxpr/convert_element_type | solution.py:94
  133.3 3.6 copy.93
  136.9 4.1 fusion.91
  143.2 2.3 fusion.88
  145.5 2.7 copy.91
  148.2 2.0 fusion.89
  150.2 1.9 constant_dynamic-update-slice_fusion.2
  152.1 3.5 fusion.90
  155.6 3.2 convolution_convert_fusion.3
  158.8 6.5 %copy.92 = bf16[2048,1024]{0,1:T(8,128)(2,1)} copy(bf16[2048,1024]{1,0:T(8,128)(2,1)} %convolution_convert_fusion.3) | data formatting | bytes 8388608 | tf_op jit(solution)/shard_map/while/body/eval_jaxpr/convert_element_type | solution.py:94
  165.4 3.6 copy.93
  169.0 4.1 fusion.91
  175.2 2.3 fusion.88
  177.5 2.7 copy.91
  180.2 2.0 fusion.89
  182.2 1.9 constant_dynamic-update-slice_fusion.2
  184.1 3.5 fusion.90
  187.7 3.2 convolution_convert_fusion.3
  190.8 6.5 %copy.92 = bf16[2048,1024]{0,1:T(8,128)(2,1)} copy(bf16[2048,1024]{1,0:T(8,128)(2,1)} %convolution_convert_fusion.3) | data formatting | bytes 8388608 | tf_op jit(solution)/shard_map/while/body/eval_jaxpr/convert_element_type | solution.py:94
  197.4 3.6 copy.93
  201.0 4.1 fusion.91
  207.2 5.3 %copy.47 = bf16[128,4,16,32]{3,2,1,0:T(8,128)(2,1)} copy(bf16[128,4,16,32]{0,2,3,1:T(8,128)(2,1)} %bitcast.181) | data formatting | bytes 1048576 | tf_op jit(solution)/shard_map/convert_element_type | solution.py:127
  212.5 2.0 copy.48
  214.5 1.5 reshape.119
  216.1 3.5 all-to-all-start.4
  222.2 6.0 %all-to-all-done.4 = bf16[8,2,16384]{2,1,0:T(2,128)(2,1)S(1)} async-done(((bf16[8,2,16384]{2,1,0:T(2,128)(2,1)}), bf16[8,2,16384]{2,1,0:T(2,128)(2,1)S(1)}, u32[]{:S(2)}, u32[]{:S(2)}) %all-to-all-start.4) | async-done | bytes 524320 | tf_op jit(solution)/shard_map/all_to_all | solution.py:33
  228.2 5.7 %all-to-all-start.6 = ((bf16[16,8,128,32]{2,1,3,0:T(8,128)(2,1)}), bf16[16,8,128,32]{2,1,3,0:T(8,128)(2,1)S(1)}, u32[]{:S(2)}, u32[]{:S(2)}) async-start(bf16[16,8,128,32]{2,1,3,0:T(8,128)(2,1)} %copy.51), calls=%async_computation.6 | async-start | bytes 2097152 | tf_op jit(solution)/shard_map/all_to_all | solution.py:33
  235.6 15.3 %all-to-all-done.6 = bf16[16,8,128,32]{2,1,3,0:T(8,128)(2,1)S(1)} async-done(((bf16[16,8,128,32]{2,1,3,0:T(8,128)(2,1)}), bf16[16,8,128,32]{2,1,3,0:T(8,128)(2,1)S(1)}, u32[]{:S(2)}, u32[]{:S(2)}) %all-to-all-start.6) | async-done | bytes 1048608 | tf_op jit(solution)/shard_map/all_to_all | solution.py:33
  250.9 4.4 %all-to-all-start.5 = ((bf16[16,2,1024]{2,1,0:T(2,128)(2,1)}), bf16[16,2,1024]{2,1,0:T(2,128)(2,1)S(1)}, u32[]{:S(2)}, u32[]{:S(2)}) async-start(bf16[16,2,1024]{2,1,0:T(2,128)(2,1)} %reshape.121), calls=%async_computation.5 | async-start | bytes 131072 | tf_op jit(solution)/shard_map/all_to_all | solution.py:129
  256.0 6.6 %all-to-all-done.5 = bf16[16,2,1024]{2,1,0:T(2,128)(2,1)S(1)} async-done(((bf16[16,2,1024]{2,1,0:T(2,128)(2,1)}), bf16[16,2,1024]{2,1,0:T(2,128)(2,1)S(1)}, u32[]{:S(2)}, u32[]{:S(2)}) %all-to-all-start.5) | async-done | bytes 65568 | tf_op jit(solution)/shard_map/all_to_all | solution.py:129
  262.7 3.4 all-to-all-start.7
  267.1 3.9 all-to-all-done.7
  272.1 144.7 %all-reduce.2.cloned.1.call-done = f32[1024,128]{1,0:T(8,128)} async-done(((f32[1024,128]{1,0:T(8,128)}), f32[1024,128]{1,0:T(8,128)}) %all-reduce.2.cloned.1.call-update) | async-done | bytes 524304 | tf_op jit(solution)/shard_map/psum | solution.py:132
  416.8 1.9 copy.112
  (123 shorter events, 28.0 us)
Async XLA Ops:
  7.2 1.9 copy-start
  14.4 16.7 %all-to-all-start = ((bf16[16,2,1024]{2,1,0:T(2,128)(2,1)}), bf16[16,2,1024]{2,1,0:T(2,128)(2,1)S(1)}, u32[]{:S(2)}, u32[]{:S(2)}) async-start(bf16[16,2,1024]{2,1,0:T(2,128)(2,1)} %reshape.113), calls=%async_computation | async-start | bytes 131072 | tf_op jit(solution)/shard_map/all_to_all | solution.py:67
  31.0 9.6 %all-to-all-start.2 = ((bf16[8,2,2048]{2,1,0:T(2,128)(2,1)}), bf16[8,2,2048]{2,1,0:T(2,128)(2,1)S(1)}, u32[]{:S(2)}, u32[]{:S(2)}) async-start(bf16[8,2,2048]{2,1,0:T(2,128)(2,1)} %reshape.117), calls=%async_computation.2 | async-start | bytes 131072 | tf_op jit(solution)/shard_map/all_to_all | solution.py:69
  36.3 23.5 %copy-start.9 = (bf16[1024,128]{1,0:T(8,128)(2,1)S(1)}, bf16[1024,128]{1,0:T(8,128)(2,1)}, u32[]{:S(2)}) copy-start(bf16[1024,128]{1,0:T(8,128)(2,1)} %param.9) | copy-start | bytes 786436
  36.3 23.7 %copy-start.11 = (bf16[128]{0:T(256)(128)(2,1)S(1)}, bf16[128]{0:T(256)(128)(2,1)}, u32[]{:S(2)}) copy-start(bf16[128]{0:T(256)(128)(2,1)} %param.10) | copy-start | bytes 772
  40.6 11.2 %all-to-all-start.1 = ((bf16[8,2,16384]{2,1,0:T(2,128)(2,1)}), bf16[8,2,16384]{2,1,0:T(2,128)(2,1)S(1)}, u32[]{:S(2)}, u32[]{:S(2)}) async-start(bf16[8,2,16384]{2,1,0:T(2,128)(2,1)} %reshape.115), calls=%async_computation.1 | async-start | bytes 1048576 | tf_op jit(solution)/shard_map/all_to_all | solution.py:10
  53.0 24.0 %all-to-all-start.3 = ((bf16[16,8,128,32]{2,1,3,0:T(8,128)(2,1)}), bf16[16,8,128,32]{2,1,3,0:T(8,128)(2,1)}, u32[]{:S(2)}, u32[]{:S(2)}) async-start(bf16[16,8,128,32]{2,1,3,0:T(8,128)(2,1)} %broadcast_in_dim.48), calls=%async_computation.3 | async-start | bytes 2097152 | tf_op jit(solution)/shard_map/all_to_all | solution.py:10
  79.1 5.1 %copy-start.2 = (bf16[128,128,32]{1,0,2:T(8,128)(2,1)}, bf16[128,128,32]{1,0,2:T(8,128)(2,1)S(1)}, u32[]{:S(2)}) copy-start(bf16[128,128,32]{1,0,2:T(8,128)(2,1)S(1)} %get-tuple-element.269) | copy-start | bytes 3145732 | tf_op jit(solution)/shard_map/while
  81.4 2.7 copy-start.10
  84.1 4.0 copy-start.1
  84.2 3.9 copy-start.7
  91.6 3.2 copy-start.8
  104.9 4.1 copy-start.3
  104.9 4.1 copy-start.5
  110.4 0.8 copy-start.6
  111.2 5.0 %copy-start.2 = (bf16[128,128,32]{1,0,2:T(8,128)(2,1)}, bf16[128,128,32]{1,0,2:T(8,128)(2,1)S(1)}, u32[]{:S(2)}) copy-start(bf16[128,128,32]{1,0,2:T(8,128)(2,1)S(1)} %get-tuple-element.269) | copy-start | bytes 3145732 | tf_op jit(solution)/shard_map/while
  113.4 2.7 copy-start.10
  116.2 4.0 copy-start.1
  116.2 3.9 copy-start.7
  123.6 3.2 copy-start.8
  136.9 4.1 copy-start.3
  136.9 4.1 copy-start.5
  142.4 0.8 copy-start.6
  143.2 5.0 %copy-start.2 = (bf16[128,128,32]{1,0,2:T(8,128)(2,1)}, bf16[128,128,32]{1,0,2:T(8,128)(2,1)S(1)}, u32[]{:S(2)}) copy-start(bf16[128,128,32]{1,0,2:T(8,128)(2,1)S(1)} %get-tuple-element.269) | copy-start | bytes 3145732 | tf_op jit(solution)/shard_map/while
  145.4 2.7 copy-start.10
  148.2 4.0 copy-start.1
  148.2 3.9 copy-start.7
  155.6 3.2 copy-start.8
  168.9 4.1 copy-start.3
  169.0 4.1 copy-start.5
  174.4 0.8 copy-start.6
  175.2 5.0 %copy-start.2 = (bf16[128,128,32]{1,0,2:T(8,128)(2,1)}, bf16[128,128,32]{1,0,2:T(8,128)(2,1)S(1)}, u32[]{:S(2)}) copy-start(bf16[128,128,32]{1,0,2:T(8,128)(2,1)S(1)} %get-tuple-element.269) | copy-start | bytes 3145732 | tf_op jit(solution)/shard_map/while
  177.5 2.7 copy-start.10
  180.2 4.0 copy-start.1
  180.2 3.9 copy-start.7
  187.6 3.2 copy-start.8
  201.0 4.1 copy-start.3
  201.0 4.1 copy-start.5
  206.4 0.8 copy-start.6
  216.1 12.1 %all-to-all-start.4 = ((bf16[8,2,16384]{2,1,0:T(2,128)(2,1)}), bf16[8,2,16384]{2,1,0:T(2,128)(2,1)S(1)}, u32[]{:S(2)}, u32[]{:S(2)}) async-start(bf16[8,2,16384]{2,1,0:T(2,128)(2,1)} %reshape.119), calls=%async_computation.4 | async-start | bytes 1048576 | tf_op jit(solution)/shard_map/all_to_all | solution.py:33
  222.2 48.9 %copy-start.4 = (bf16[1,1024,64]{1,2,0:T(8,128)(2,1)S(1)}, bf16[1,1024,64]{1,2,0:T(8,128)(2,1)}, u32[]{:S(2)}) copy-start(bf16[1,1024,64]{1,2,0:T(8,128)(2,1)} %param.7) | copy-start | bytes 393220
  228.2 22.7 %all-to-all-start.6 = ((bf16[16,8,128,32]{2,1,3,0:T(8,128)(2,1)}), bf16[16,8,128,32]{2,1,3,0:T(8,128)(2,1)S(1)}, u32[]{:S(2)}, u32[]{:S(2)}) async-start(bf16[16,8,128,32]{2,1,3,0:T(8,128)(2,1)} %copy.51), calls=%async_computation.6 | async-start | bytes 2097152 | tf_op jit(solution)/shard_map/all_to_all | solution.py:33
  250.9 11.8 %all-to-all-start.5 = ((bf16[16,2,1024]{2,1,0:T(2,128)(2,1)}), bf16[16,2,1024]{2,1,0:T(2,128)(2,1)S(1)}, u32[]{:S(2)}, u32[]{:S(2)}) async-start(bf16[16,2,1024]{2,1,0:T(2,128)(2,1)} %reshape.121), calls=%async_computation.5 | async-start | bytes 131072 | tf_op jit(solution)/shard_map/all_to_all | solution.py:129
  262.7 8.4 %all-to-all-start.7 = ((bf16[8,128,32]{1,2,0:T(8,128)(2,1)}), bf16[8,128,32]{1,2,0:T(8,128)(2,1)S(1)}, u32[]{:S(2)}, u32[]{:S(2)}) async-start(bf16[8,128,32]{1,2,0:T(8,128)(2,1)} %copy.53), calls=%async_computation.7 | async-start | bytes 131072 | tf_op jit(solution)/shard_map/all_to_all | solution.py:131
  266.0 150.8 %all-reduce.2.cloned.1.call-start = ((), (), s32[]{:S(2)}) async-start(), calls=%async_computation.8 | async-start | bytes 1048576 | tf_op jit(solution)/shard_map/psum | solution.py:132
Sparse Core Ops, SparseCore 0:
  272.2 144.5 all-reduce.1
where the time goes:
time: 428 us; the launch traced here: 426 us
  waiting for transfers between devices  199 us (46%)
  local copies, waits for them, and re-layouts  96.1 us (22%)
  matrix products  66.7 us (16%)
  starting transfers between devices  41.1 us (10%)
  between operations  14.4 us (3%)
  other arithmetic  7.57 us (2%)
    psum x1, waiting for transfers between devices, on_device(): factor_weight_gradient = lax.psum(weight_part, ('row', 'col'))  145 us
    convert_element_type x4, local copies, waits for them, and re-layouts, advance(): jnp.dot(grad_rows, weight_back, preferred_element_type=jnp.float32)  26.1 us
    all_to_all x2, waiting for transfers between devices, summed_on_arrival(): pieces = lax.all_to_all(cut_along(array, dim, size), axis, 0, 0, tiled=True)  21.3 us
    while x68, local copies, waits for them, and re-layouts  17.6 us
    dot_general x4, matrix products, advance(): jnp.einsum('ijce,sic->sje', outer_grad, left_block, preferred_element_typ...  16.3 us
    unnamed x25, local copies, waits for them, and re-layouts  15.8 us
    all_to_all x2, waiting for transfers between devices, copy_for_each(): lax.all_to_all(jnp.broadcast_to(array[None], (size, *array.shape)), axis,...  15.2 us
    dot_general x4, matrix products, advance(): lax.dot_general(flat, grad_rows, (((0,), (0,)), ((), ())), preferred_elem...  14 us
  transfers between devices with their start and end apart: 9, of which 9 were waited for; matrix products, arithmetic and copies ran while one was open for 5% of the time, Pallas kernels for 0%

commit v1 on v0

--- a/solution.py
+++ b/solution.py
@@ -3,6 +3,7 @@
 import jax.numpy as jnp
 from jax import lax
 from jax.sharding import PartitionSpec as P
+from jax.lax import psum
 
 
 def copy_for_each(array, axis):
@@ -129,7 +130,7 @@
     left_back = lax.all_to_all(left_summed, "row", split_axis=0, concat_axis=1, tiled=True)
     right_summed = summed_on_arrival(right_grad.astype(jnp.bfloat16), "row", 0).astype(jnp.bfloat16)
     right_back = lax.all_to_all(right_summed, "col", split_axis=0, concat_axis=1, tiled=True)
-    factor_weight_gradient = lax.psum(weight_part, ("row", "col"))
+    factor_weight_gradient = psum(psum(weight_part, "row"), "col")
     both = jnp.concatenate([left_back, right_back], axis=-1)
     normalized_gradient = jnp.dot(both, split_mapping_matrix.T, preferred_element_type=jnp.float32)
     first_factor = jnp.mean(normalized_gradient, axis=-1, keepdims=True)

time: 428 us -> 466 us (1.089)
  waiting for transfers between devices: 199 us -> 232 us
    psum x1 -> x2, waiting for transfers between devices: 145 us -> 183 us  [on_device(): factor_weight_gradient = psum(psum(weight_part, 'row'), 'col')]
  transfers between devices with their start and end apart: 9 -> 10, of which waited for: 9 -> 9; matrix products, arithmetic and copies ran while one was open for 5% -> 5% of each run, Pallas kernels for 0% -> 0%
where the time goes in v1:
time: 466 us; the launch traced here: 459 us
  waiting for transfers between devices  232 us (50%)
  local copies, waits for them, and re-layouts  96.1 us (21%)
  matrix products  66.7 us (14%)
  starting transfers between devices  41.2 us (9%)
  between operations  14.4 us (3%)
  other arithmetic  7.57 us (2%)
    psum x2, waiting for transfers between devices, on_device(): factor_weight_gradient = psum(psum(weight_part, 'row'), 'col')  183 us
    convert_element_type x4, local copies, waits for them, and re-layouts, advance(): jnp.dot(grad_rows, weight_back, preferred_element_type=jnp.float32)  26.1 us
    all_to_all x2, waiting for transfers between devices, summed_on_arrival(): pieces = lax.all_to_all(cut_along(array, dim, size), axis, 0, 0, tiled=True)  20.6 us
    while x68, local copies, waits for them, and re-layouts  17.6 us
    dot_general x4, matrix products, advance(): jnp.einsum('ijce,sic->sje', outer_grad, left_block, preferred_element_typ...  16.3 us
    unnamed x25, local copies, waits for them, and re-layouts  15.8 us
    all_to_all x2, waiting for transfers between devices, copy_for_each(): lax.all_to_all(jnp.broadcast_to(array[None], (size, *array.shape)), axis,...  15.2 us
    dot_general x4, matrix products, advance(): lax.dot_general(flat, grad_rows, (((0,), (0,)), ((), ())), preferred_elem...  14 us
  transfers between devices with their start and end apart: 10, of which 9 were waited for; matrix products, arithmetic and copies ran while one was open for 5% of the time, Pallas kernels for 0%

profile of v1, /device:TPU:1, one launch (start us, length us, event | category | flops | bytes accessed | tf_op | source)
XLA Modules:
  0.0 459.0 jit_solution(9826051068119240061)
XLA Ops:
  11.2 2.3 reduce.7
  14.4 9.3 %all-to-all-start = ((bf16[16,2,1024]{2,1,0:T(2,128)(2,1)}), bf16[16,2,1024]{2,1,0:T(2,128)(2,1)S(1)}, u32[]{:S(2)}, u32[]{:S(2)}) async-start(bf16[16,2,1024]{2,1,0:T(2,128)(2,1)} %reshape.113), calls=%async_computation | async-start | bytes 131072 | tf_op jit(solution)/shard_map/all_to_all | solution.py:68
  24.0 2.3 reduce.8
  27.2 3.8 all-to-all-done
  31.0 4.5 all-to-all-start.2
  36.5 1.5 reshape.115
  38.0 2.6 all-to-all-done.2
  40.6 3.5 all-to-all-start.1
  44.8 7.0 %all-to-all-done.1 = bf16[8,2,16384]{2,1,0:T(2,128)(2,1)S(1)} async-done(((bf16[8,2,16384]{2,1,0:T(2,128)(2,1)}), bf16[8,2,16384]{2,1,0:T(2,128)(2,1)S(1)}, u32[]{:S(2)}, u32[]{:S(2)}) %all-to-all-start.1) | async-done | bytes 524320 | tf_op jit(solution)/shard_map/all_to_all | solution.py:11
  53.0 6.9 %all-to-all-start.3 = ((bf16[16,8,128,32]{2,1,3,0:T(8,128)(2,1)}), bf16[16,8,128,32]{2,1,3,0:T(8,128)(2,1)}, u32[]{:S(2)}, u32[]{:S(2)}) async-start(bf16[16,8,128,32]{2,1,3,0:T(8,128)(2,1)} %broadcast_in_dim.48), calls=%async_computation.3 | async-start | bytes 2097152 | tf_op jit(solution)/shard_map/all_to_all | solution.py:11
  60.0 1.6 reshape.116
  63.0 1.9 copy.40
  64.9 3.9 copy.45
  68.8 8.3 %all-to-all-done.3 = bf16[16,8,128,32]{2,1,3,0:T(8,128)(2,1)} async-done(((bf16[16,8,128,32]{2,1,3,0:T(8,128)(2,1)}), bf16[16,8,128,32]{2,1,3,0:T(8,128)(2,1)}, u32[]{:S(2)}, u32[]{:S(2)}) %all-to-all-start.3) | async-done | bytes 1048608 | tf_op jit(solution)/shard_map/all_to_all | solution.py:11
  78.9 128.3 %while.17 = (s32[]{:T(128)}, f32[1024,128]{1,0:T(8,128)}, f32[128,128,32]{1,0,2:T(8,128)S(1)}, bf16[4,16,128,128]{3,2,1,0:T(8,128)(2,1)}, bf16[4,128,16,32]{1,2,...) while((s32[]{:T(128)}, f32[1024,128]{1,0:T(8,128)}, ...), condition=%wide.region_3.4_spmd.clone, body=%wide.region_2.3_spmd.clone.sunk | while | flops 3229941760 | bytes 96995688 | solution.py:122
  79.1 2.3 fusion.88
  81.4 2.7 copy.91
  84.2 2.0 fusion.89
  86.2 1.9 constant_dynamic-update-slice_fusion.2
  88.1 3.5 fusion.90
  91.6 3.2 convolution_convert_fusion.3
  94.8 6.5 %copy.92 = bf16[2048,1024]{0,1:T(8,128)(2,1)} copy(bf16[2048,1024]{1,0:T(8,128)(2,1)} %convolution_convert_fusion.3) | data formatting | bytes 8388608 | tf_op jit(solution)/shard_map/while/body/eval_jaxpr/convert_element_type | solution.py:95
  101.3 3.6 copy.93
  104.9 4.1 fusion.91
  111.2 2.3 fusion.88
  113.4 2.7 copy.91
  116.2 2.0 fusion.89
  118.2 1.9 constant_dynamic-update-slice_fusion.2
  120.1 3.5 fusion.90
  123.6 3.2 convolution_convert_fusion.3
  126.8 6.5 %copy.92 = bf16[2048,1024]{0,1:T(8,128)(2,1)} copy(bf16[2048,1024]{1,0:T(8,128)(2,1)} %convolution_convert_fusion.3) | data formatting | bytes 8388608 | tf_op jit(solution)/shard_map/while/body/eval_jaxpr/convert_element_type | solution.py:95
  133.3 3.6 copy.93
  136.9 4.1 fusion.91
  143.2 2.3 fusion.88
  145.5 2.7 copy.91
  148.2 2.0 fusion.89
  150.2 1.9 constant_dynamic-update-slice_fusion.2
  152.1 3.5 fusion.90
  155.6 3.2 convolution_convert_fusion.3
  158.8 6.5 %copy.92 = bf16[2048,1024]{0,1:T(8,128)(2,1)} copy(bf16[2048,1024]{1,0:T(8,128)(2,1)} %convolution_convert_fusion.3) | data formatting | bytes 8388608 | tf_op jit(solution)/shard_map/while/body/eval_jaxpr/convert_element_type | solution.py:95
  165.4 3.6 copy.93
  169.0 4.1 fusion.91
  175.2 2.3 fusion.88
  177.5 2.7 copy.91
  180.2 2.0 fusion.89
  182.2 1.9 constant_dynamic-update-slice_fusion.2
  184.1 3.5 fusion.90
  187.7 3.2 convolution_convert_fusion.3
  190.8 6.5 %copy.92 = bf16[2048,1024]{0,1:T(8,128)(2,1)} copy(bf16[2048,1024]{1,0:T(8,128)(2,1)} %convolution_convert_fusion.3) | data formatting | bytes 8388608 | tf_op jit(solution)/shard_map/while/body/eval_jaxpr/convert_element_type | solution.py:95
  197.4 3.6 copy.93
  201.0 4.1 fusion.91
  207.2 5.3 %copy.47 = bf16[128,4,16,32]{3,2,1,0:T(8,128)(2,1)} copy(bf16[128,4,16,32]{0,2,3,1:T(8,128)(2,1)} %bitcast.181) | data formatting | bytes 1048576 | tf_op jit(solution)/shard_map/convert_element_type | solution.py:128
  212.5 2.0 copy.48
  214.5 1.5 reshape.119
  216.1 3.5 all-to-all-start.4
  222.2 6.0 %all-to-all-done.4 = bf16[8,2,16384]{2,1,0:T(2,128)(2,1)S(1)} async-done(((bf16[8,2,16384]{2,1,0:T(2,128)(2,1)}), bf16[8,2,16384]{2,1,0:T(2,128)(2,1)S(1)}, u32[]{:S(2)}, u32[]{:S(2)}) %all-to-all-start.4) | async-done | bytes 524320 | tf_op jit(solution)/shard_map/all_to_all | solution.py:34
  228.2 5.7 %all-to-all-start.6 = ((bf16[16,8,128,32]{2,1,3,0:T(8,128)(2,1)}), bf16[16,8,128,32]{2,1,3,0:T(8,128)(2,1)S(1)}, u32[]{:S(2)}, u32[]{:S(2)}) async-start(bf16[16,8,128,32]{2,1,3,0:T(8,128)(2,1)} %copy.51), calls=%async_computation.6 | async-start | bytes 2097152 | tf_op jit(solution)/shard_map/all_to_all | solution.py:34
  236.3 14.6 %all-to-all-done.6 = bf16[16,8,128,32]{2,1,3,0:T(8,128)(2,1)S(1)} async-done(((bf16[16,8,128,32]{2,1,3,0:T(8,128)(2,1)}), bf16[16,8,128,32]{2,1,3,0:T(8,128)(2,1)S(1)}, u32[]{:S(2)}, u32[]{:S(2)}) %all-to-all-start.6) | async-done | bytes 1048608 | tf_op jit(solution)/shard_map/all_to_all | solution.py:34
  250.9 4.4 all-to-all-start.5
  256.1 6.7 %all-to-all-done.5 = bf16[16,2,1024]{2,1,0:T(2,128)(2,1)S(1)} async-done(((bf16[16,2,1024]{2,1,0:T(2,128)(2,1)}), bf16[16,2,1024]{2,1,0:T(2,128)(2,1)S(1)}, u32[]{:S(2)}, u32[]{:S(2)}) %all-to-all-start.5) | async-done | bytes 65568 | tf_op jit(solution)/shard_map/all_to_all | solution.py:130
  262.7 3.4 all-to-all-start.7
  266.5 110.5 %all-reduce.3.cloned.1.call-done = f32[1024,128]{1,0:T(8,128)} async-done(((f32[1024,128]{1,0:T(8,128)}), f32[1024,128]{1,0:T(8,128)}) %all-reduce.3.cloned.1.call-update) | async-done | bytes 524304 | tf_op jit(solution)/shard_map/psum | solution.py:133
  378.1 72.2 %all-reduce.5.cloned.1.call-done = f32[1024,128]{1,0:T(8,128)} async-done(((f32[1024,128]{1,0:T(8,128)}), f32[1024,128]{1,0:T(8,128)}) %all-reduce.5.cloned.1.call-update) | async-done | bytes 524304 | tf_op jit(solution)/shard_map/psum | solution.py:133
  450.2 1.9 copy.113
  (126 shorter events, 28.0 us)
Async XLA Ops:
  7.2 1.9 copy-start
  14.4 16.7 %all-to-all-start = ((bf16[16,2,1024]{2,1,0:T(2,128)(2,1)}), bf16[16,2,1024]{2,1,0:T(2,128)(2,1)S(1)}, u32[]{:S(2)}, u32[]{:S(2)}) async-start(bf16[16,2,1024]{2,1,0:T(2,128)(2,1)} %reshape.113), calls=%async_computation | async-start | bytes 131072 | tf_op jit(solution)/shard_map/all_to_all | solution.py:68
  31.0 9.6 %all-to-all-start.2 = ((bf16[8,2,2048]{2,1,0:T(2,128)(2,1)}), bf16[8,2,2048]{2,1,0:T(2,128)(2,1)S(1)}, u32[]{:S(2)}, u32[]{:S(2)}) async-start(bf16[8,2,2048]{2,1,0:T(2,128)(2,1)} %reshape.117), calls=%async_computation.2 | async-start | bytes 131072 | tf_op jit(solution)/shard_map/all_to_all | solution.py:70
  36.3 23.5 %copy-start.9 = (bf16[1024,128]{1,0:T(8,128)(2,1)S(1)}, bf16[1024,128]{1,0:T(8,128)(2,1)}, u32[]{:S(2)}) copy-start(bf16[1024,128]{1,0:T(8,128)(2,1)} %param.9) | copy-start | bytes 786436
  36.3 23.7 %copy-start.11 = (bf16[128]{0:T(256)(128)(2,1)S(1)}, bf16[128]{0:T(256)(128)(2,1)}, u32[]{:S(2)}) copy-start(bf16[128]{0:T(256)(128)(2,1)} %param.10) | copy-start | bytes 772
  40.6 11.2 %all-to-all-start.1 = ((bf16[8,2,16384]{2,1,0:T(2,128)(2,1)}), bf16[8,2,16384]{2,1,0:T(2,128)(2,1)S(1)}, u32[]{:S(2)}, u32[]{:S(2)}) async-start(bf16[8,2,16384]{2,1,0:T(2,128)(2,1)} %reshape.115), calls=%async_computation.1 | async-start | bytes 1048576 | tf_op jit(solution)/shard_map/all_to_all | solution.py:11
  53.0 24.0 %all-to-all-start.3 = ((bf16[16,8,128,32]{2,1,3,0:T(8,128)(2,1)}), bf16[16,8,128,32]{2,1,3,0:T(8,128)(2,1)}, u32[]{:S(2)}, u32[]{:S(2)}) async-start(bf16[16,8,128,32]{2,1,3,0:T(8,128)(2,1)} %broadcast_in_dim.48), calls=%async_computation.3 | async-start | bytes 2097152 | tf_op jit(solution)/shard_map/all_to_all | solution.py:11
  79.1 5.1 %copy-start.2 = (bf16[128,128,32]{1,0,2:T(8,128)(2,1)}, bf16[128,128,32]{1,0,2:T(8,128)(2,1)S(1)}, u32[]{:S(2)}) copy-start(bf16[128,128,32]{1,0,2:T(8,128)(2,1)S(1)} %get-tuple-element.269) | copy-start | bytes 3145732 | tf_op jit(solution)/shard_map/while
  81.4 2.7 copy-start.10
  84.1 4.0 copy-start.1
  84.2 3.9 copy-start.7
  91.6 3.2 copy-start.8
  104.9 4.1 copy-start.3
  104.9 4.1 copy-start.5
  110.4 0.8 copy-start.6
  111.2 5.0 %copy-start.2 = (bf16[128,128,32]{1,0,2:T(8,128)(2,1)}, bf16[128,128,32]{1,0,2:T(8,128)(2,1)S(1)}, u32[]{:S(2)}) copy-start(bf16[128,128,32]{1,0,2:T(8,128)(2,1)S(1)} %get-tuple-element.269) | copy-start | bytes 3145732 | tf_op jit(solution)/shard_map/while
  113.4 2.7 copy-start.10
  116.2 4.0 copy-start.1
  116.2 3.9 copy-start.7
  123.6 3.2 copy-start.8
  136.9 4.1 copy-start.3
  136.9 4.1 copy-start.5
  142.4 0.8 copy-start.6
  143.2 5.0 %copy-start.2 = (bf16[128,128,32]{1,0,2:T(8,128)(2,1)}, bf16[128,128,32]{1,0,2:T(8,128)(2,1)S(1)}, u32[]{:S(2)}) copy-start(bf16[128,128,32]{1,0,2:T(8,128)(2,1)S(1)} %get-tuple-element.269) | copy-start | bytes 3145732 | tf_op jit(solution)/shard_map/while
  145.4 2.7 copy-start.10
  148.2 4.0 copy-start.1
  148.2 3.9 copy-start.7
  155.6 3.2 copy-start.8
  168.9 4.1 copy-start.3
  169.0 4.1 copy-start.5
  174.4 0.8 copy-start.6
  175.2 5.0 %copy-start.2 = (bf16[128,128,32]{1,0,2:T(8,128)(2,1)}, bf16[128,128,32]{1,0,2:T(8,128)(2,1)S(1)}, u32[]{:S(2)}) copy-start(bf16[128,128,32]{1,0,2:T(8,128)(2,1)S(1)} %get-tuple-element.269) | copy-start | bytes 3145732 | tf_op jit(solution)/shard_map/while
  177.5 2.7 copy-start.10
  180.2 4.0 copy-start.1
  180.2 3.9 copy-start.7
  187.6 3.2 copy-start.8
  201.0 4.1 copy-start.3
  201.0 4.1 copy-start.5
  206.4 0.8 copy-start.6
  216.1 12.1 %all-to-all-start.4 = ((bf16[8,2,16384]{2,1,0:T(2,128)(2,1)}), bf16[8,2,16384]{2,1,0:T(2,128)(2,1)S(1)}, u32[]{:S(2)}, u32[]{:S(2)}) async-start(bf16[8,2,16384]{2,1,0:T(2,128)(2,1)} %reshape.119), calls=%async_computation.4 | async-start | bytes 1048576 | tf_op jit(solution)/shard_map/all_to_all | solution.py:34
  222.2 154.9 %copy-start.4 = (bf16[1,1024,64]{1,2,0:T(8,128)(2,1)S(1)}, bf16[1,1024,64]{1,2,0:T(8,128)(2,1)}, u32[]{:S(2)}) copy-start(bf16[1,1024,64]{1,2,0:T(8,128)(2,1)} %param.7) | copy-start | bytes 393220
  228.2 22.7 %all-to-all-start.6 = ((bf16[16,8,128,32]{2,1,3,0:T(8,128)(2,1)}), bf16[16,8,128,32]{2,1,3,0:T(8,128)(2,1)S(1)}, u32[]{:S(2)}, u32[]{:S(2)}) async-start(bf16[16,8,128,32]{2,1,3,0:T(8,128)(2,1)} %copy.51), calls=%async_computation.6 | async-start | bytes 2097152 | tf_op jit(solution)/shard_map/all_to_all | solution.py:34
  233.9 143.1 %all-reduce.3.cloned.1.call-start = ((), (), s32[]{:S(2)}) async-start(), calls=%async_computation.8 | async-start | bytes 1048576 | tf_op jit(solution)/shard_map/psum | solution.py:133
  250.9 11.8 %all-to-all-start.5 = ((bf16[16,2,1024]{2,1,0:T(2,128)(2,1)}), bf16[16,2,1024]{2,1,0:T(2,128)(2,1)S(1)}, u32[]{:S(2)}, u32[]{:S(2)}) async-start(bf16[16,2,1024]{2,1,0:T(2,128)(2,1)} %reshape.121), calls=%async_computation.5 | async-start | bytes 131072 | tf_op jit(solution)/shard_map/all_to_all | solution.py:130
  262.7 114.3 %all-to-all-start.7 = ((bf16[8,128,32]{1,2,0:T(8,128)(2,1)}), bf16[8,128,32]{1,2,0:T(8,128)(2,1)S(1)}, u32[]{:S(2)}, u32[]{:S(2)}) async-start(bf16[8,128,32]{1,2,0:T(8,128)(2,1)} %copy.53), calls=%async_computation.7 | async-start | bytes 131072 | tf_op jit(solution)/shard_map/all_to_all | solution.py:132
  266.1 184.2 %all-reduce.5.cloned.1.call-start = ((), (), s32[]{:S(2)}) async-start(), calls=%async_computation.9 | async-start | bytes 1048576 | tf_op jit(solution)/shard_map/psum | solution.py:133
Sparse Core Ops, SparseCore 0:
  237.8 139.1 all-reduce.2
  379.5 70.7 all-reduce.4
